TPU v7x, 32 devices: a whole 2x2x4 slice. The times are simulated.
32 devices in a mesh: feat: 8 (over y, x, core), rep: 4 (over z).
Axes of the slice: x: 2, y: 2, z: 4, core: 2. Of those that a mesh axis runs over, the one named last changes fastest.
Arguments:
- features: bfloat16 [4, 8, 1024, 512], P('rep', None, 'feat'), may hold values from -6 to 6
- adjacency_one: int32 [4, 8, 5, 16, 512], P('rep'), may hold values from 0 to 65535, as said below
- pre_hidden: bfloat16 [4, 8, 256, 256], P('rep', 'feat'), may hold values from -6 to 6
- adjacency_two: int32 [4, 8, 5, 8, 256], P('rep', 'feat'), may hold values from 0 to 65535, as said below
- weight_two: bfloat16 [6, 256, 256], replicated, may hold values from -0.375 to 0.375
- out_grad: bfloat16 [4, 8, 128, 256], P('rep', 'feat'), may hold values from -6 to 6
Outputs:
- grad_w1: float32 [6, 1024, 256], P(None, 'feat')
- grad_b1: float32 [256], replicated
- grad_w2: float32 [6, 256, 256], replicated
- grad_b2: float32 [256], replicated
Inputs may be any that keep to these rules, and one draw needn't show every extreme that they name: `adjacency_one`: bit k, k below 16, of word (w, n) is the entry of destination row 16 w + k and source column n; higher bits are zero; some rows are empty. `adjacency_two`: bit k, k below 16, of word (w, n) is the entry of seed row 16 w + k and source column n; higher bits are zero; some rows are empty.
All inputs are finite; a program needn't handle non-finite values.
Results may differ from a plain program's by a relative error of at most 0.0041.
Values may be sent and summed in bfloat16 or wider, within the bound.
No kernel may reach another device: no remote copies, remote signals or barrier semaphores. Data moves between devices by JAX's collectives and lax.ppermute only.
A program may use at most 128 MiB of HBM per device.

v0:
```python
import math
import jax
import jax.numpy as jnp
from jax import lax
from jax.sharding import PartitionSpec as P


def unpack(packed):
    shifts = jnp.arange(16, dtype=jnp.int32)
    spread = jnp.bitwise_and(jnp.right_shift(packed[..., None, :], shifts[:, None]), 1)
    dense = spread.reshape(packed.shape[:-2] + (packed.shape[-2] * 16, packed.shape[-1]))
    degree = jnp.sum(dense, axis=-1).astype(jnp.float32)
    return (dense.astype(jnp.bfloat16), 1.0 / jnp.maximum(degree, 1.0))


def upper_layer(pre_rows, words_two, grad_rows, weight_two, factor):
    hidden = jnp.maximum(pre_rows, 0)
    seed_count = grad_rows.shape[0]
    matrix, inverse = unpack(words_two)
    mixed = (
        jnp.einsum("rsd,dh->rsh", matrix, hidden, preferred_element_type=jnp.float32)
        * inverse[..., None]
    ).astype(jnp.bfloat16)
    scaled = grad_rows.astype(jnp.float32) * factor
    scaled_low = scaled.astype(jnp.bfloat16)
    grad_rel = jnp.einsum("rsh,sk->rhk", mixed, scaled_low, preferred_element_type=jnp.float32)
    grad_self = jnp.einsum(
        "sh,sk->hk", hidden[:seed_count], scaled_low, preferred_element_type=jnp.float32
    )
    weight_grad = jnp.concatenate([grad_self[None], grad_rel], 0)
    backed = (
        jnp.einsum("sk,rhk->rsh", scaled_low, weight_two[1:], preferred_element_type=jnp.float32)
        * inverse[..., None]
    ).astype(jnp.bfloat16)
    spread_back = jnp.einsum("rsd,rsh->dh", matrix, backed, preferred_element_type=jnp.float32)
    own_part = jnp.einsum(
        "sk,hk->sh", scaled_low, weight_two[0], preferred_element_type=jnp.float32
    )
    hidden_total = spread_back + jnp.pad(own_part, ((0, hidden.shape[0] - seed_count), (0, 0)))
    hidden_grad = jnp.where(pre_rows > 0, hidden_total, 0.0).astype(jnp.bfloat16)
    return (
        weight_grad,
        jnp.sum(scaled, 0),
        hidden_grad,
        jnp.sum(hidden_grad.astype(jnp.float32), 0),
    )


def panel_terms(word_block, column_block, grad_block):
    matrix, inverse = unpack(word_block)
    rows_one = grad_block.shape[1]
    gathered = (
        jnp.einsum("brdn,bcn->brdc", matrix, column_block, preferred_element_type=jnp.float32)
        * inverse[..., None]
    ).astype(jnp.bfloat16)
    panel_rel = jnp.einsum(
        "brdc,bdh->rch", gathered, grad_block, preferred_element_type=jnp.float32
    )
    panel_self = jnp.einsum(
        "bcd,bdh->ch", column_block[:, :, :rows_one], grad_block, preferred_element_type=jnp.float32
    )
    return jnp.concatenate([panel_self[None], panel_rel], 0)


def on_device(features, adjacency_one, pre_hidden, adjacency_two, weight_two, out_grad):
    seed_count = out_grad.shape[2]
    factor = float(seed_count * lax.axis_size("feat") * lax.axis_size("rep")) ** (-0.5)
    weight_grad, bias_two, hidden_grad, bias_one = upper_layer(
        pre_hidden[0, 0], adjacency_two[0, 0], out_grad[0, 0], weight_two, factor
    )
    feature_local = features[0]
    adj_local = adjacency_one[0]
    col_width = feature_local.shape[1]
    hidden_width = hidden_grad.shape[1]
    relations = adj_local.shape[1]
    initial = jnp.zeros((relations + 1, col_width, hidden_width), jnp.float32)
    piece = lax.all_gather(hidden_grad[None], "feat", axis=0, tiled=True)
    piece_rows = piece.shape[0]
    group_size = math.gcd(piece_rows, 8)
    turn_count = piece_rows // group_size
    word_block = adj_local
    word_block = word_block.reshape((turn_count, group_size) + adj_local.shape[1:])
    column_block = feature_local
    column_block = column_block.reshape((turn_count, group_size) + feature_local.shape[1:])
    grad_block = piece.reshape((turn_count, group_size) + piece.shape[1:])

    def one_turn(running, inputs):
        return (running + panel_terms(inputs[0], inputs[1], inputs[2]), None)

    running, unused = lax.scan(one_turn, initial, (word_block, column_block, grad_block))
    grad_w1 = lax.psum(running, "rep")
    grad_w2, grad_b1, grad_b2 = lax.psum((weight_grad, bias_one, bias_two), ("feat", "rep"))
    return (grad_w1, grad_b1, grad_w2, grad_b2)


def solution(mesh):
    placed = (
        P("rep", None, "feat", None),
        P("rep", None, None, None, None),
        P("rep", "feat", None, None),
        P("rep", "feat", None, None, None),
        P(),
        P("rep", "feat", None, None),
    )
    return jax.shard_map(
        on_device,
        mesh=mesh,
        in_specs=placed,
        out_specs=(P(None, "feat", None), P(), P(), P()),
        check_vma=False,
    )
```

profile of v0, /device:TPU:0, one launch (start us, length us, event | category | flops | bytes accessed | tf_op | source)
XLA Modules:
  0.0 213.1 jit_solution(5158156742498113044)
XLA Ops:
  8.0 0.0 copy-start
  8.0 0.0 all-gather.3.cloned.1.call-start
  8.1 1.6 fusion.28
  9.7 0.1 div.22
  9.8 0.1 shift_right_arithmetic.72
  9.9 0.9 fusion.27
  10.8 1.1 fusion.37
  11.9 2.4 %convert_reduce_fusion = (f32[256]{0:T(256)S(1)}, bf16[256,256]{1,0:T(8,128)(2,1)}) fusion(f32[128,256]{1,0:T(8,128)S(1)} %fusion.37, bf16[5,128,256]{2,1,0:T(8,128)(2,1)S(1)} %fusion.27, bf16[6,256,256]{2,1,0:T(8,128)(2,1)} %param.10, f32[5,128]{1,0:T(8,128)S(1)} %div.22, bf16[1,1,128,256]{3,2,1,0:T(8,128)(2,1)} %param.11, bf16[1,1,256,256]{3,2,1,0:T(8,128)(2,1)} %param.8), kind=kOutput, calls=%fused_computation.38 | convolution fusion | flops 168722176 | bytes 1445376 | tf_op jit(solution)/shard_map/rsd,rsh->dh/dot_general | solution.py:35
  14.4 0.0 all-gather.3.cloned.1.call-update
  14.4 0.0 all-reduce.7.cloned.1.call-start
  14.4 0.9 broadcast_maximum_fusion
  15.4 1.0 convolution_bitcast_fusion.1
  16.4 1.6 fusion.19
  18.0 1.2 pad_maximum_fusion
  19.3 0.0 all-reduce.7.cloned.1.call-update
  19.3 0.2 all-reduce.5.cloned.1.call-start
  19.5 0.0 copy-done
  19.5 10.9 %and_reduce_fusion = s32[8,5,16,16]{3,2,1,0:T(8,128)S(1)} fusion(s32[8,5,16,512]{3,2,1,0:T(8,128)S(1)} %bitcast.90), kind=kLoop, calls=%fused_computation.3 | loop fusion | flops 15718400 | bytes 1351680 | tf_op jit(solution)/shard_map/while/body/eval_jaxpr/reduce_sum | solution.py:12
  30.4 0.1 maximum_divide_fusion
  30.5 0.2 reshape.90
  30.7 0.1 shift_right_arithmetic.81
  30.7 10.1 %all-gather.3.cloned.1.call-done = bf16[2048,256]{1,0:T(8,128)(2,1)} async-done(((bf16[256,256]{1,0:T(8,128)(2,1)}), bf16[2048,256]{1,0:T(8,128)(2,1)}) %all-gather.3.cloned.1.call-update) | async-done | bytes 1048592 | tf_op jit(solution)/shard_map/all_gather | solution.py:77
  40.9 0.0 copy-start.2
  40.9 0.0 copy-start.3
  40.9 10.5 %shift_right_arithmetic.78 = s32[8,5,16,16,512]{4,3,2,1,0:T(8,128)} broadcast(s32[8,5,16,512]{3,2,1,0:T(8,128)S(1)} %bitcast.91), dimensions={0,1,2,4} | broadcast | bytes 22282240 | tf_op jit(solution)/shard_map/while/body/eval_jaxpr/shift_right_arithmetic | solution.py:10
  51.3 0.0 copy-done.2
  51.3 0.0 copy-done.3
  51.3 0.0 copy-start.1
  51.3 9.5 %fusion.13 = f32[5,128,256]{2,1,0:T(8,128)S(1)} fusion(bf16[8,256,256,1]{2,1,0,3:T(8,128)(2,1)S(1)} %bitcast.96, f32[8,5,256]{2,0,1:T(8,128)S(1)} %copy.37, s32[8,5,256,512]{3,2,1,0:T(8,128)} %bitcast.89, s32[256]{0:T(256)S(1)} %shift_right_arithmetic.81, bf16[1,8,128,512]{3,2,1,0:T(8,128)(2,1)S(1)} %copy-done.2), kind=kOutput, calls=%fused_computation.14 | convolution fusion | flops 2031616000 | bytes 23766016 | tf_op jit(solution)/shard_map/while/body/eval_jaxpr/brdc,bdh->rch/dot_general | solution.py:56
  60.8 0.5 convolution_bitcast_fusion.2
  61.3 0.1 copy.30
  61.4 1.0 pad_maximum_fusion.1
  62.4 0.0 all-reduce.5.cloned.1.call-update
  62.4 0.0 copy-done.1
  62.4 39.3 %all-reduce.1 = (f32[256]{0:T(256)}, f32[256]{0:T(256)}) all-reduce(f32[256]{0:T(256)S(1)} %get-tuple-element.23, f32[256]{0:T(256)S(1)} %fusion.40), channel_id=1, replica_groups=mesh['feat'=8,'rep'=4] {'feat','rep'}, use_global_device_ids=true, to_apply=%region_4.5 | all-reduce | flops 512 | bytes 4096 | tf_op jit(solution)/shard_map/psum | solution.py:92
  101.8 53.7 %all-reduce.7.cloned.1.call-done = f32[6,256,256]{2,1,0:T(8,128)} async-done(((f32[6,256,256]{2,1,0:T(8,128)}), f32[6,256,256]{2,1,0:T(8,128)}) %all-reduce.7.cloned.1.call-update) | async-done | bytes 1572880 | tf_op jit(solution)/shard_map/psum | solution.py:92
  155.4 45.4 %all-reduce.5.cloned.1.call-done = f32[6,128,256]{2,1,0:T(8,128)} async-done(((f32[6,128,256]{2,1,0:T(8,128)}), f32[6,128,256]{2,1,0:T(8,128)}) %all-reduce.5.cloned.1.call-update) | async-done | bytes 786448 | tf_op jit(solution)/shard_map/psum | solution.py:91
  200.8 2.1 copy.52
  202.9 2.7 %copy.53 = f32[6,256,256]{2,1,0:T(8,128)} copy(f32[6,256,256]{2,1,0:T(8,128)} %all-reduce.7.cloned.1.call-done) | data formatting | bytes 3145728
  (5 shorter events, 0.1 us)
Async XLA Ops:
  8.0 11.5 %copy-start = (s32[1,8,5,16,512]{4,3,2,1,0:T(8,128)S(1)}, s32[1,8,5,16,512]{4,3,2,1,0:T(8,128)}, u32[]{:S(2)}) copy-start(s32[1,8,5,16,512]{4,3,2,1,0:T(8,128)} %param.7) | copy-start | bytes 3932164
  8.0 32.9 %all-gather.3.cloned.1.call-start = ((), (), s32[]{:S(2)}) async-start(), calls=%async_computation.2 | async-start | bytes 1179648 | tf_op jit(solution)/shard_map/all_gather | solution.py:77
  14.4 141.0 %all-reduce.7.cloned.1.call-start = ((), (), s32[]{:S(2)}) async-start(), calls=%async_computation.1 | async-start | bytes 3145728 | tf_op jit(solution)/shard_map/psum | solution.py:92
  19.3 181.5 %all-reduce.5.cloned.1.call-start = ((), (), s32[]{:S(2)}) async-start(), calls=%async_computation | async-start | bytes 1572864 | tf_op jit(solution)/shard_map/psum | solution.py:91
  40.9 10.5 %copy-start.2 = (bf16[1,8,128,512]{3,2,1,0:T(8,128)(2,1)S(1)}, bf16[1,8,128,512]{3,2,1,0:T(8,128)(2,1)}, u32[]{:S(2)}) copy-start(bf16[1,8,128,512]{3,2,1,0:T(8,128)(2,1)} %param.6) | copy-start | bytes 3145732
  40.9 10.5 %copy-start.3 = (bf16[2048,256]{1,0:T(8,128)(2,1)S(1)}, bf16[2048,256]{1,0:T(8,128)(2,1)}, u32[]{:S(2)}) copy-start(bf16[2048,256]{1,0:T(8,128)(2,1)} %all-gather.3.cloned.1.call-done) | copy-start | bytes 3145732
  51.3 11.0 %copy-start.1 = (bf16[1,1,128,256]{3,2,1,0:T(8,128)(2,1)S(1)}, bf16[1,1,128,256]{3,2,1,0:T(8,128)(2,1)}, u32[]{:S(2)}) copy-start(bf16[1,1,128,256]{3,2,1,0:T(8,128)(2,1)} %param.11) | copy-start | bytes 196612
Sparse Core Ops, SparseCore 0:
  14.5 26.3 all-gather.2
Sparse Core Ops, SparseCore 1:
  20.7 134.6 all-reduce.6
  158.2 42.5 all-reduce.4
where the time goes:
time: 214 us; the launch traced here: 213 us
  waiting for transfers between devices  109 us (51%)
  blocking collectives  39.3 us (18%)
  other arithmetic  16.6 us (8%)
  matrix products  16.1 us (8%)
  local copies, waits for them, and re-layouts  15.8 us (7%)
  between operations  15.6 us (7%)
    psum x1, waiting for transfers between devices, on_device(): lax.psum((weight_grad, bias_one, bias_two), ('feat', 'rep'))  53.7 us
    psum x1, waiting for transfers between devices, on_device(): grad_w1 = lax.psum(running, 'rep')  45.4 us
    psum x1, blocking collectives, on_device(): lax.psum((weight_grad, bias_one, bias_two), ('feat', 'rep'))  39.3 us
    reduce_sum x1, other arithmetic, unpack(): degree = jnp.sum(dense, axis=-1).astype(jnp.float32)  10.9 us
    shift_right_arithmetic x5, local copies, waits for them, and re-layouts, unpack(): jnp.right_shift(packed[..., None, :], shifts[:, None])  10.6 us
    all_gather x1, waiting for transfers between devices, on_device(): piece = lax.all_gather(hidden_grad[None], 'feat', axis=0, tiled=True)  10.1 us
    dot_general x1, matrix products, panel_terms(): jnp.einsum('brdc,bdh->rch', gathered, grad_block, preferred_element_type=...  9.46 us
    unnamed x10, local copies, waits for them, and re-layouts  4.85 us
  transfers between devices with their start and end apart: 3, of which 3 were waited for; matrix products, arithmetic and copies ran while one was open for 18% of the time, Pallas kernels for 0%

commit v1 on v0

--- a/solution.py
+++ b/solution.py
@@ -3,6 +3,12 @@
 import jax.numpy as jnp
 from jax import lax
 from jax.sharding import PartitionSpec as P
+from jax.lax import all_gather
+
+
+def _obtain_words(local_x):
+    y_new = jnp.sum(all_gather(local_x, "rep"), 0)
+    return y_new
 
 
 def unpack(packed):
@@ -88,7 +94,7 @@
         return (running + panel_terms(inputs[0], inputs[1], inputs[2]), None)
 
     running, unused = lax.scan(one_turn, initial, (word_block, column_block, grad_block))
-    grad_w1 = lax.psum(running, "rep")
+    grad_w1 = _obtain_words(running)
     grad_w2, grad_b1, grad_b2 = lax.psum((weight_grad, bias_one, bias_two), ("feat", "rep"))
     return (grad_w1, grad_b1, grad_w2, grad_b2)
 

time: 214 us -> 244 us (1.14)
  waiting for transfers between devices: 109 us -> 141 us
  local copies, waits for them, and re-layouts: 15.8 us -> 3.27 us
  other arithmetic: 16.6 us -> 26.3 us
  blocking collectives: 39.3 us -> 44 us
  matrix products: 16.1 us -> 13.2 us
    psum x1, waiting for transfers between devices: 53.7 us -> 113 us  [on_device(): lax.psum((weight_grad, bias_one, bias_two), ('feat', 'rep'))]
    psum x1 -> x0, waiting for transfers between devices: 45.4 us -> none  [on_device(): grad_w1 = lax.psum(running, 'rep')]
    all_gather x0 -> x1, waiting for transfers between devices: none -> 20.6 us  [_obtain_words(): y_new = jnp.sum(all_gather(local_x, 'rep'), 0)]
    shift_right_arithmetic x5 -> x4, local copies, waits for them, and re-layouts: 10.6 us -> 0.17 us  [unpack(): jnp.right_shift(packed[..., None, :], shifts[:, None])]
    convert_element_type x2 -> x3, other arithmetic: 2.55 us -> 9.85 us  [unpack(): return (dense.astype(jnp.bfloat16), 1.0 / jnp.maximum(degree, 1.0))]
    psum x1, blocking collectives: 39.3 us -> 44 us  [on_device(): lax.psum((weight_grad, bias_one, bias_two), ('feat', 'rep'))]
    reduce_sum x0 -> x1, other arithmetic: none -> 3.07 us  [_obtain_words(): y_new = jnp.sum(all_gather(local_x, 'rep'), 0)]
    all_gather x1, waiting for transfers between devices: 10.1 us -> 7.53 us  [on_device(): piece = lax.all_gather(hidden_grad[None], 'feat', axis=0, tiled=True)]
  transfers between devices with their start and end apart: 3 -> 3, of which waited for: 3 -> 3; matrix products, arithmetic and copies ran while one was open for 18% -> 10% of each run, Pallas kernels for 0% -> 0%
where the time goes in v1:
time: 244 us
  waiting for transfers between devices  141 us (58%)
  blocking collectives  44 us (18%)
  other arithmetic  26.3 us (11%)
  between operations  15.6 us (6%)
  matrix products  13.2 us (5%)
  local copies, waits for them, and re-layouts  3.27 us (1%)
    psum x1, waiting for transfers between devices, on_device(): lax.psum((weight_grad, bias_one, bias_two), ('feat', 'rep'))  113 us
    psum x1, blocking collectives, on_device(): lax.psum((weight_grad, bias_one, bias_two), ('feat', 'rep'))  44 us
    all_gather x1, waiting for transfers between devices, _obtain_words(): y_new = jnp.sum(all_gather(local_x, 'rep'), 0)  20.6 us
    reduce_sum x1, other arithmetic, unpack(): degree = jnp.sum(dense, axis=-1).astype(jnp.float32)  11 us
    convert_element_type x3, other arithmetic, unpack(): return (dense.astype(jnp.bfloat16), 1.0 / jnp.maximum(degree, 1.0))  9.85 us
    all_gather x1, waiting for transfers between devices, on_device(): piece = lax.all_gather(hidden_grad[None], 'feat', axis=0, tiled=True)  7.53 us
    dot_general x1, matrix products, panel_terms(): jnp.einsum('brdc,bdh->rch', gathered, grad_block, preferred_element_type=...  7.01 us
  transfers between devices with their start and end apart: 3, of which 3 were waited for; matrix products, arithmetic and copies ran while one was open for 10% of the time, Pallas kernels for 0%

profile of v1, /device:TPU:0, one launch (start us, length us, event | category | flops | bytes accessed | tf_op | source)
XLA Modules:
  0.0 243.7 jit_solution(4107933674266037306)
XLA Ops:
  8.0 0.0 copy-start
  8.0 0.0 all-gather.5.cloned.1.call-start
  8.1 1.6 fusion.20
  9.7 0.1 div.22
  9.8 0.1 shift_right_arithmetic.72
  9.9 0.9 fusion.19
  10.8 1.1 fusion.29
  11.9 2.4 convert_reduce_fusion
  14.4 0.0 all-gather.5.cloned.1.call-update
  14.4 0.0 all-gather.7.cloned.1.call-start
  14.5 0.1 shift_right_arithmetic.81
  14.5 0.0 copy-done
  14.5 7.3 %fusion.1 = bf16[8,5,256,512]{3,2,0,1:T(8,128)(2,1)} fusion(s32[256]{0:T(256)S(1)} %shift_right_arithmetic.81, s32[1,8,5,16,512]{4,3,2,1,0:T(8,128)S(1)} %copy-done), kind=kLoop, calls=%fused_computation.2 | loop fusion | flops 15728640 | bytes 11797504 | tf_op jit(solution)/shard_map/while/body/eval_jaxpr/convert_element_type | solution.py:19
  21.8 0.0 copy-start.3
  21.8 11.0 %and_reduce_fusion = s32[8,5,16,16]{3,2,0,1:T(8,128)S(1)} fusion(s32[1,8,5,16,512]{4,3,2,1,0:T(8,128)S(1)} %copy-done), kind=kLoop, calls=%fused_computation.3 | loop fusion | flops 15718400 | bytes 1351680 | tf_op jit(solution)/shard_map/while/body/eval_jaxpr/reduce_sum | solution.py:18
  32.9 0.1 maximum_divide_fusion
  32.9 0.2 div.24
  33.1 7.5 %all-gather.5.cloned.1.call-done = bf16[2048,256]{1,0:T(8,128)(2,1)} async-done(((bf16[256,256]{1,0:T(8,128)(2,1)}), bf16[2048,256]{1,0:T(8,128)(2,1)}) %all-gather.5.cloned.1.call-update) | async-done | bytes 1048592 | tf_op jit(solution)/shard_map/all_gather | solution.py:83
  40.7 0.0 copy-done.3
  40.7 1.7 convolution_bitcast_fusion.2
  42.4 0.1 copy.22
  42.5 0.0 copy-start.2
  42.5 7.0 %fusion.6 = f32[5,128,256]{2,1,0:T(8,128)S(1)} fusion(bf16[8,256,256,1]{2,1,0,3:T(8,128)(2,1)} %bitcast.110, f32[8,5,256]{2,0,1:T(8,128)S(1)} %div.24, bf16[8,5,256,512]{3,2,0,1:T(8,128)(2,1)} %fusion.1, bf16[1,8,128,512]{3,2,1,0:T(8,128)(2,1)} %param.6), kind=kOutput, calls=%fused_computation.9 | convolution fusion | flops 2015887360 | bytes 13279232 | tf_op jit(solution)/shard_map/while/body/eval_jaxpr/brdc,bdh->rch/dot_general | solution.py:62
  49.5 0.0 copy-start.1
  49.5 0.9 pad_maximum_fusion.1
  50.4 0.0 all-gather.7.cloned.1.call-update
  50.5 0.0 all-reduce.4.cloned.1.call-start
  50.5 0.0 copy-done.2
  50.5 0.0 copy-done.1
  50.5 0.2 convolution_bitcast_fusion.1
  50.8 0.7 fusion.11
  51.5 1.2 pad_maximum_fusion
  52.7 0.0 all-reduce.4.cloned.1.call-update
  52.8 44.0 %all-reduce.1 = (f32[256]{0:T(256)}, f32[256]{0:T(256)}) all-reduce(f32[256]{0:T(256)S(1)} %get-tuple-element.23, f32[256]{0:T(256)S(1)} %fusion.32), channel_id=1, replica_groups=mesh['feat'=8,'rep'=4] {'feat','rep'}, use_global_device_ids=true, to_apply=%region_4.5 | all-reduce | flops 512 | bytes 4096 | tf_op jit(solution)/shard_map/psum | solution.py:98
  96.7 20.6 %all-gather.7.cloned.1.call-done = f32[24,128,256]{2,1,0:T(8,128)} async-done(((f32[6,128,256]{2,1,0:T(8,128)}), f32[24,128,256]{2,1,0:T(8,128)}) %all-gather.7.cloned.1.call-update) | async-done | bytes 3145744 | tf_op jit(solution)/shard_map/all_gather | solution.py:10
  117.3 3.1 %reduce_sum.48 = f32[6,128,256]{2,1,0:T(8,128)} reduce(f32[4,6,128,256]{3,2,1,0:T(8,128)} %bitcast.104, f32[]{:T(128)} %constant.13.clone.1), dimensions={0}, to_apply=%region_2.3 | reduce | flops 589824 | bytes 3932164 | tf_op jit(solution)/shard_map/reduce_sum | solution.py:10
  120.4 113.2 %all-reduce.4.cloned.1.call-done = f32[6,256,256]{2,1,0:T(8,128)} async-done(((f32[6,256,256]{2,1,0:T(8,128)}), f32[6,256,256]{2,1,0:T(8,128)}) %all-reduce.4.cloned.1.call-update) | async-done | bytes 1572880 | tf_op jit(solution)/shard_map/psum | solution.py:98
  233.5 2.7 %copy.34 = f32[6,256,256]{2,1,0:T(8,128)} copy(f32[6,256,256]{2,1,0:T(8,128)} %all-reduce.4.cloned.1.call-done) | data formatting | bytes 3145728
  (5 shorter events, 0.1 us)
Async XLA Ops:
  8.0 6.5 %copy-start = (s32[1,8,5,16,512]{4,3,2,1,0:T(8,128)S(1)}, s32[1,8,5,16,512]{4,3,2,1,0:T(8,128)}, u32[]{:S(2)}) copy-start(s32[1,8,5,16,512]{4,3,2,1,0:T(8,128)} %param.7) | copy-start | bytes 3932164
  8.0 32.6 %all-gather.5.cloned.1.call-start = ((), (), s32[]{:S(2)}) async-start(), calls=%async_computation.1 | async-start | bytes 1179648 | tf_op jit(solution)/shard_map/all_gather | solution.py:83
  14.4 102.9 %all-gather.7.cloned.1.call-start = ((), (), s32[]{:S(2)}) async-start(), calls=%async_computation.2 | async-start | bytes 3932160 | tf_op jit(solution)/shard_map/all_gather | solution.py:10
  21.8 18.8 %copy-start.3 = (bf16[1,8,128,512]{3,2,1,0:T(8,128)(2,1)S(1)}, bf16[1,8,128,512]{3,2,1,0:T(8,128)(2,1)}, u32[]{:S(2)}) copy-start(bf16[1,8,128,512]{3,2,1,0:T(8,128)(2,1)} %param.6) | copy-start | bytes 3145732
  42.5 8.1 %copy-start.2 = (bf16[1,1,256,256]{3,2,1,0:T(8,128)(2,1)S(1)}, bf16[1,1,256,256]{3,2,1,0:T(8,128)(2,1)}, u32[]{:S(2)}) copy-start(bf16[1,1,256,256]{3,2,1,0:T(8,128)(2,1)} %param.8) | copy-start | bytes 393220
  49.5 1.1 copy-start.1
  50.5 183.1 %all-reduce.4.cloned.1.call-start = ((), (), s32[]{:S(2)}) async-start(), calls=%async_computation | async-start | bytes 3145728 | tf_op jit(solution)/shard_map/psum | solution.py:98
Sparse Core Ops, SparseCore 0:
  14.5 26.0 all-gather.4
  50.6 66.6 all-gather.6
Sparse Core Ops, SparseCore 1:
  56.8 176.7 all-reduce.3
